TPU v7x, 32 devices: a whole 2x2x4 slice. The times are simulated.
32 devices in a mesh: runs: 2 (over x), space: 16 (over z, y, core).
Axes of the slice: x: 2, y: 2, z: 4, core: 2. Of those that a mesh axis runs over, the one named last changes fastest.
Arguments:
- levels: float32 [4, 24, 32, 16, 128], P('runs', None, 'space'), parts along dimension 0, may hold values from -6 to 6
- region_offset: int32 [6], P('runs'), parts along dimension 0, may hold values from 0 to 127, as said below
- advect: float32 [3, 24, 24], replicated, may hold values from -1 to 1
- coupling: float32 [24, 24], replicated, may hold values from -0.8 to 0.8
- diffusion: float32 [24], replicated, may hold values from 0.02 to 0.15
Outputs:
- levels_out: float32 [4, 24, 32, 16, 128], P('runs', None, 'space'), parts along dimension 0
There are 2 independent parts, one for each index of `runs`. A program takes and returns all parts, laid end to end along the dimension named above; an argument that names none is the same for every part. Nothing has to cross between parts.
Inputs may be any that keep to these rules, and one draw needn't show every extreme that they name: `region_offset`: the first entry lies in 0 to 31, the second in 0 to 15, the third in 0 to 127; the refined box may wrap around the periodic coarse grid.
All inputs are finite; a program needn't handle non-finite values.
Results may differ from a plain program's by a relative error of at most 0.0001.
Values sent between devices are 32-bit elements; how exact they have to be, the bound alone decides.
A program may use at most 128 MiB of HBM per device.

v0:
```python
from functools import partial

import jax
import jax.numpy as jnp
from jax import lax
from jax.sharding import PartitionSpec as P

coarse_step = 0.25
coarse_spacing = 1.0
damping = 0.2
fractions = (0.0, 0.5, 0.5, 1.0)
highest = lax.Precision.HIGHEST


def padded_2(x, sides, width, wrap):
    for axis, dim in sides:
        devices, length = (lax.axis_size(axis), x.shape[dim])
        up = [(i, (i + 1) % devices) for i in range(devices if wrap else devices - 1)]
        down = [(j, i) for i, j in up]
        last = lax.slice_in_dim(x, length - width, length, axis=dim)
        first = lax.slice_in_dim(x, 0, width, axis=dim)
        before = lax.ppermute(last, axis, up)
        after = lax.ppermute(first, axis, down)
        x = jnp.concatenate([before, x, after], axis=dim)
    return x


def stencil_terms(padded, dimension, length, spacing):
    shifted = [lax.slice_in_dim(padded, k, k + length, axis=dimension) for k in range(5)]
    gradient = (shifted[0] - 8.0 * shifted[1] + 8.0 * shifted[3] - shifted[4]) / (12.0 * spacing)
    second = (16.0 * (shifted[1] + shifted[3]) - shifted[0] - shifted[4] - 30.0 * shifted[2]) / (
        12.0 * spacing * spacing
    )
    fourth = shifted[0] + shifted[4] - 4.0 * (shifted[1] + shifted[3]) + 6.0 * shifted[2]
    return (gradient, second, fourth)


def tendency(fields, padded, spacing, mixing, diffusion):
    stencils = [stencil_terms(padded[d - 1], d, fields.shape[d], spacing) for d in (1, 2, 3)]
    stacked = jnp.concatenate([stencils[0][0], stencils[1][0], stencils[2][0], fields], axis=0)
    coupled = jnp.einsum("fg,gxyz->fxyz", mixing, stacked, precision=highest)
    second = stencils[0][1] + stencils[1][1] + stencils[2][1]
    fourth = stencils[0][2] + stencils[1][2] + stencils[2][2]
    return coupled + diffusion[:, None, None, None] * second - damping / (16.0 * spacing) * fourth


def advance(fields, timestep, evaluate):
    rate_one = evaluate(fields, 0)
    rate_two = evaluate(fields + 0.5 * timestep * rate_one, 1)
    rate_three = evaluate(fields + 0.5 * timestep * rate_two, 2)
    rate_four = evaluate(fields + timestep * rate_three, 3)
    return fields + timestep / 6.0 * (rate_one + 2.0 * rate_two + 2.0 * rate_three + rate_four)


def mixing_matrix(advect, coupling):
    symmetric = 0.5 * (advect + jnp.swapaxes(advect, 1, 2))
    return jnp.concatenate([symmetric[0], symmetric[1], symmetric[2], coupling], axis=1)


def hat_weights(fine_index, coarse_index):
    location = 0.5 * fine_index.astype(jnp.float32)[:, None] + 0.75
    return jnp.maximum(0.0, 1.0 - jnp.abs(location - coarse_index.astype(jnp.float32)[None, :]))


def wrap_pad(fields, dimension):
    length = fields.shape[dimension]
    low_rim = lax.slice_in_dim(fields, length - 2, length, axis=dimension)
    high_rim = lax.slice_in_dim(fields, 0, 2, axis=dimension)
    return jnp.concatenate([low_rim, fields, high_rim], axis=dimension)


def with_ghosts(fields, ghost, dimension):
    return jnp.concatenate(
        [
            lax.slice_in_dim(ghost, 0, 2, axis=dimension),
            fields,
            lax.slice_in_dim(ghost, 2, 4, axis=dimension),
        ],
        axis=dimension,
    )


def prolong(weights_across, weights_rows, weights_depth, source):
    return jnp.einsum(
        "ai,bj,ck,fijk->fabc",
        weights_across,
        weights_rows,
        weights_depth,
        source,
        precision=highest,
    )


def into_window(select, source):
    return jnp.einsum("wk,fkyz->fwyz", select, source, precision=highest)


def near_rows(source, dimension, half_count):
    return jnp.concatenate(
        [
            lax.slice_in_dim(source, 0, 3, axis=dimension),
            lax.slice_in_dim(source, half_count + 1, half_count + 4, axis=dimension),
        ],
        axis=dimension,
    )


def skin_index(half_count):
    return jnp.concatenate(
        [jnp.arange(3, dtype=jnp.int32), half_count + 1 + jnp.arange(3, dtype=jnp.int32)]
    )


def ghost_index(length):
    return jnp.concatenate(
        [jnp.arange(2, dtype=jnp.int32), length + 2 + jnp.arange(2, dtype=jnp.int32)]
    )


def local(levels, region_offset, advect, coupling, diffusion):
    mixing = mixing_matrix(advect, coupling)
    coarse_level = levels[0]
    fine_level = levels[1]
    fields_count = coarse_level.shape[0]
    planes = coarse_level.shape[1]
    rows_count = coarse_level.shape[2]
    depth_count = coarse_level.shape[3]
    devices = lax.axis_size("space")
    position = lax.axis_index("space")
    total_across = planes * devices
    half_across = total_across // 2
    half_rows = rows_count // 2
    half_depth = depth_count // 2
    half_planes = planes // 2
    offset_across = region_offset[0]
    offset_rows = region_offset[1]
    offset_depth = region_offset[2]

    def coarse_rate(fields, section_index):
        across = padded_2(fields, (("space", 1),), 2, True)
        padded = [across, wrap_pad(fields, 2), wrap_pad(fields, 3)]
        return tendency(fields, padded, coarse_spacing, mixing, diffusion)

    coarse_new = advance(coarse_level, coarse_step, coarse_rate)
    global_across = position * planes + jnp.arange(planes, dtype=jnp.int32)
    window_across = jnp.mod(
        offset_across - 2 + jnp.arange(half_across + 4, dtype=jnp.int32), total_across
    )
    select = (window_across[:, None] == global_across[None, :]).astype(jnp.float32)

    def local_box(fields):
        rolled = jnp.roll(fields, (2 - offset_rows, 2 - offset_depth), axis=(2, 3))
        return rolled[:, :, : half_rows + 4, : half_depth + 4]

    window_start = position * half_planes + 1

    def cut_parts(skins):
        rows_skin, depth_skin, ends_skin = skins
        rows_part = lax.dynamic_slice_in_dim(rows_skin, window_start, half_planes + 2, axis=1)
        depth_part = lax.dynamic_slice_in_dim(depth_skin, window_start, half_planes + 2, axis=1)
        return (rows_part, depth_part, ends_skin)

    box_old = local_box(coarse_level)
    box_new = local_box(coarse_new)
    ends_select = near_rows(select, 0, half_across)
    rows_old = into_window(select, near_rows(box_old, 2, half_rows))
    depth_old = into_window(select, near_rows(box_old, 3, half_depth))
    ends_old = into_window(ends_select, box_old)
    rows_new = into_window(select, near_rows(box_new, 2, half_rows))
    depth_new = into_window(select, near_rows(box_new, 3, half_depth))
    ends_new = into_window(ends_select, box_new)
    summed = lax.psum((rows_old, depth_old, ends_old, rows_new, depth_new, ends_new), "space")
    parts_old = cut_parts(summed[:3])
    parts_new = cut_parts(summed[3:])
    interior_across = hat_weights(
        position * planes + 2 + jnp.arange(planes, dtype=jnp.int32),
        window_start + jnp.arange(half_planes + 2, dtype=jnp.int32),
    )
    interior_rows = hat_weights(
        2 + jnp.arange(rows_count, dtype=jnp.int32), jnp.arange(half_rows + 4, dtype=jnp.int32)
    )
    interior_depth = hat_weights(
        2 + jnp.arange(depth_count, dtype=jnp.int32), jnp.arange(half_depth + 4, dtype=jnp.int32)
    )
    exterior_across = hat_weights(ghost_index(total_across), skin_index(half_across))
    exterior_rows = hat_weights(ghost_index(rows_count), skin_index(half_rows))
    exterior_depth = hat_weights(ghost_index(depth_count), skin_index(half_depth))

    def ghost_layers(parts):
        rows_part, depth_part, ends_skin = parts
        return (
            prolong(exterior_across, interior_rows, interior_depth, ends_skin),
            prolong(interior_across, exterior_rows, interior_depth, rows_part),
            prolong(interior_across, interior_rows, exterior_depth, depth_part),
        )

    ghosts_old = ghost_layers(parts_old)
    ghosts_new = ghost_layers(parts_new)

    def fine_rate(fields, section_index, substep):
        weight = (substep + fractions[section_index]) * 0.5
        ghosts = [
            (1.0 - weight) * before_step + weight * after_step
            for before_step, after_step in zip(ghosts_old, ghosts_new)
        ]
        across = padded_2(fields, (("space", 1),), 2, False)
        low_side = jnp.where(position == 0, ghosts[0][:, :2], across[:, :2])
        high_side = jnp.where(position == devices - 1, ghosts[0][:, 2:], across[:, planes + 2 :])
        across = jnp.concatenate([low_side, across[:, 2 : planes + 2], high_side], axis=1)
        padded = [across, with_ghosts(fields, ghosts[1], 2), with_ghosts(fields, ghosts[2], 3)]
        return tendency(fields, padded, 0.5 * coarse_spacing, mixing, diffusion)

    for substep in range(2):
        fine_level = advance(fine_level, 0.5 * coarse_step, partial(fine_rate, substep=substep))
    restricted = fine_level.reshape(fields_count, half_planes, 2, half_rows, 2, half_depth, 2).mean(
        axis=(2, 4, 6)
    )
    relative = jnp.mod(global_across - offset_across, total_across)
    arrived = lax.all_gather(restricted, "space", axis=1, tiled=True)
    length = arrived.shape[1]
    chosen = (relative[:, None] == jnp.arange(length, dtype=jnp.int32)[None, :]).astype(jnp.float32)
    landed = jnp.einsum("km,fmyz->fkyz", chosen, arrived, precision=highest)
    padded_block = jnp.pad(
        landed, ((0, 0), (0, 0), (0, rows_count - half_rows), (0, depth_count - half_depth))
    )
    placed = jnp.roll(padded_block, (offset_rows, offset_depth), axis=(2, 3))
    inside_rows = (
        jnp.mod(jnp.arange(rows_count, dtype=jnp.int32) - offset_rows, rows_count) < half_rows
    )
    inside_depth = (
        jnp.mod(jnp.arange(depth_count, dtype=jnp.int32) - offset_depth, depth_count) < half_depth
    )
    inside_across = relative < half_across
    inside = inside_across[:, None, None] & inside_rows[None, :, None] & inside_depth[None, None, :]
    coarse_final = jnp.where(inside[None], placed, coarse_new)
    return jnp.stack([coarse_final, fine_level])


def solution(mesh):
    return jax.shard_map(
        local,
        mesh=mesh,
        in_specs=(P("runs", None, "space", None, None), P("runs"), P(), P(), P()),
        out_specs=P("runs", None, "space", None, None),
        check_vma=False,
    )
```

profile of v0, /device:TPU:13, one launch (start us, length us, event | category | flops | bytes accessed | tf_op | source)
XLA Modules:
  0.0 442.1 jit_solution(5654096078132212382)
XLA Ops:
  7.8 1.9 collective-permute-start
  14.4 3.4 collective-permute-done.1
  21.6 2.1 collective-permute-start.3
  26.4 4.8 %collective-permute-done.3 = f32[24,2,16,128]{3,2,1,0:T(8,128)S(1)} collective-permute-done((f32[24,2,16,128]{3,2,1,0:T(8,128)S(1)}, f32[24,2,16,128]{3,2,1,0:T(8,128)S(1)}, u32[]{:S(2)}, u32[]{:S(2)}) %collective-permute-start.3) | collective-permute-done | bytes 393248 | tf_op jit(solution)/shard_map/ppermute | solution.py:23
  34.4 15.4 %collective-permute-start.5 = (f32[24,2,16,128]{3,2,1,0:T(8,128)S(1)}, f32[24,2,16,128]{3,2,1,0:T(8,128)S(1)}, u32[]{:S(2)}, u32[]{:S(2)}) collective-permute-start(f32[24,2,16,128]{3,2,1,0:T(8,128)S(1)} %get-tuple-element.30), channel_id=1, source_target_pairs={{1,0},{2,1},{3,2},{4,3},{5,4},{6,5},{7,6},{8,7},{9,8},{10,9},{11,1... | collective-permute-start | bytes 1179656 | tf_op jit(solution)/shard_map/ppermute | solution.py:23
  50.8 4.4 collective-permute-done.5
  60.7 2.3 collective-permute-done.6
  63.1 5.1 %collective-permute-done.7 = f32[24,2,16,128]{3,2,1,0:T(8,128)S(1)} collective-permute-done((f32[24,2,16,128]{3,2,1,0:T(8,128)S(1)}, f32[24,2,16,128]{3,2,1,0:T(8,128)S(1)}, u32[]{:S(2)}, u32[]{:S(2)}) %collective-permute-start.7) | collective-permute-done | bytes 393248 | tf_op jit(solution)/shard_map/ppermute | solution.py:23
  73.2 2.1 convolution_bitcast_fusion
  75.4 2.1 convolution_bitcast_fusion.1
  80.1 2.9 convolution_bitcast_fusion.2
  83.0 2.3 convolution_bitcast_fusion.3
  85.3 1.8 convolution_bitcast_fusion.5
  87.2 1.8 convolution_bitcast_fusion.4
  89.0 1.9 collective-permute-start.8
  91.0 5.4 %collective-permute-start.9 = (f32[24,2,16,128]{3,2,1,0:T(8,128)S(1)}, f32[24,2,16,128]{3,2,1,0:T(8,128)}, u32[]{:S(2)}, u32[]{:S(2)}) collective-permute-start(f32[24,2,16,128]{3,2,1,0:T(8,128)S(1)} %get-tuple-element.61), channel_id=1, source_target_pairs={{1,0},{2,1},{3,2},{4,3},{5,4},{6,5},{7,6},{8,7},{9,8},{10,9},{11,1... | collective-permute-start | bytes 1179656 | tf_op jit(solution)/shard_map/ppermute | solution.py:23
  96.7 157.6 %all-reduce.4.cloned.1.call-done = (f32[24,20,12,6]{1,0,3,2:T(8,128)}, f32[24,20,12,6]{1,0,3,2:T(8,128)}, f32[24,20,6,68]{3,1,2,0:T(8,128)}, f32[24,20,6,68]{3,1...) async-done(((f32[24,20,12,6]{1,0,3,2:T(8,128)}, f32[24,20,12,6]{1,0,3,2:T(8,128)}, f32[24,20,6,68]{3,1,2,0:T(8,128)}, f32[24,20,6,68]{3,1,2,0:T(8,128)}, ...) | async-done | bytes 2783248 | tf_op jit(solution)/shard_map/psum | solution.py:172
  254.2 2.1 fusion.141
  256.3 2.0 fusion.143
  264.3 1.7 fusion.30
  266.0 4.5 %fusion.28 = f32[24,12,6,2]{0,3,2,1:T(2,128)S(1)} fusion(f32[24,20,12,6]{1,0,3,2:T(8,128)S(1)} %copy-done.12, s32[]{:T(128)S(6)} %select_n.149, f32[3]{0:T(128)S(1)} %add_convert_fusion.6, f32[2]{0:T(128)S(1)} %multiply_add_fusion.17), kind=kOutput, calls=%fused_computation.48 | convolution fusion | flops 124440 | bytes 152088 | tf_op jit(solution)/shard_map/ai,bj,ck,fijk->fabc/dot_general | solution.py:84
  270.5 1.7 convolution_bitcast_fusion.7
  273.2 4.5 %fusion.26 = f32[24,12,6,2]{0,3,2,1:T(2,128)S(1)} fusion(f32[24,20,12,6]{1,0,3,2:T(8,128)S(1)} %copy-done.11, s32[]{:T(128)S(6)} %select_n.149, f32[3]{0:T(128)S(1)} %add_convert_fusion.6, f32[2]{0:T(128)S(1)} %multiply_add_fusion.17), kind=kOutput, calls=%fused_computation.46 | convolution fusion | flops 124440 | bytes 152088 | tf_op jit(solution)/shard_map/ai,bj,ck,fijk->fabc/dot_general | solution.py:84
  280.3 2.0 multiply_add_fusion
  284.0 1.7 fusion.16
  286.7 4.0 collective-permute-start.10
  290.7 1.9 collective-permute-start.11
  293.7 1.8 collective-permute-done.10
  295.4 5.3 %collective-permute-done.11 = f32[24,2,16,128]{3,2,1,0:T(8,128)S(1)} collective-permute-done((f32[24,2,16,128]{3,2,1,0:T(8,128)S(1)}, f32[24,2,16,128]{3,2,1,0:T(8,128)S(1)}, u32[]{:S(2)}, u32[]{:S(2)}) %collective-permute-start.11) | collective-permute-done | bytes 393248 | tf_op jit(solution)/shard_map/ppermute | solution.py:23
  304.0 1.9 collective-permute-start.12
  306.0 2.6 collective-permute-start.13
  310.7 5.4 %collective-permute-done.13 = f32[24,2,16,128]{3,2,1,0:T(8,128)S(1)} collective-permute-done((f32[24,2,16,128]{3,2,1,0:T(8,128)S(1)}, f32[24,2,16,128]{3,2,1,0:T(8,128)S(1)}, u32[]{:S(2)}, u32[]{:S(2)}) %collective-permute-start.13) | collective-permute-done | bytes 393248 | tf_op jit(solution)/shard_map/ppermute | solution.py:23
  319.4 1.9 collective-permute-start.14
  321.4 2.7 collective-permute-start.15
  326.1 5.4 %collective-permute-done.15 = f32[24,2,16,128]{3,2,1,0:T(8,128)S(1)} collective-permute-done((f32[24,2,16,128]{3,2,1,0:T(8,128)S(1)}, f32[24,2,16,128]{3,2,1,0:T(8,128)S(1)}, u32[]{:S(2)}, u32[]{:S(2)}) %collective-permute-start.15) | collective-permute-done | bytes 393248 | tf_op jit(solution)/shard_map/ppermute | solution.py:23
  334.8 1.9 collective-permute-start.16
  336.8 4.4 collective-permute-start.17
  343.2 4.3 collective-permute-done.17
  350.8 1.9 collective-permute-start.18
  352.8 4.6 %collective-permute-start.19 = (f32[24,2,16,128]{3,2,1,0:T(8,128)S(1)}, f32[24,2,16,128]{3,2,1,0:T(8,128)S(1)}, u32[]{:S(2)}, u32[]{:S(2)}) collective-permute-start(f32[24,2,16,128]{3,2,1,0:T(8,128)S(1)} %get-tuple-element.20), channel_id=1, source_target_pairs={{1,0},{2,1},{3,2},{4,3},{5,4},{6,5},{7,6},{8,7},{9,8},{10,9},{11,1... | collective-permute-start | bytes 1179656 | tf_op jit(solution)/shard_map/ppermute | solution.py:23
  358.4 5.7 %collective-permute-done.19 = f32[24,2,16,128]{3,2,1,0:T(8,128)S(1)} collective-permute-done((f32[24,2,16,128]{3,2,1,0:T(8,128)S(1)}, f32[24,2,16,128]{3,2,1,0:T(8,128)S(1)}, u32[]{:S(2)}, u32[]{:S(2)}) %collective-permute-start.19) | collective-permute-done | bytes 393248 | tf_op jit(solution)/shard_map/ppermute | solution.py:23
  366.5 1.8 multiply_add_fusion.5
  368.3 1.9 collective-permute-start.20
  370.2 4.8 %collective-permute-start.21 = (f32[24,2,16,128]{3,2,1,0:T(8,128)S(1)}, f32[24,2,16,128]{3,2,1,0:T(8,128)}, u32[]{:S(2)}, u32[]{:S(2)}) collective-permute-start(f32[24,2,16,128]{3,2,1,0:T(8,128)S(1)} %get-tuple-element.18), channel_id=1, source_target_pairs={{1,0},{2,1},{3,2},{4,3},{5,4},{6,5},{7,6},{8,7},{9,8},{10,9},{11,1... | collective-permute-start | bytes 1179656 | tf_op jit(solution)/shard_map/ppermute | solution.py:23
  386.8 3.1 collective-permute-start.22
  389.9 2.8 collective-permute-start.23
  394.6 5.4 %collective-permute-done.23 = f32[24,2,16,128]{3,2,1,0:T(8,128)S(1)} collective-permute-done((f32[24,2,16,128]{3,2,1,0:T(8,128)S(1)}, f32[24,2,16,128]{3,2,1,0:T(8,128)S(1)}, u32[]{:S(2)}, u32[]{:S(2)}) %collective-permute-start.23) | collective-permute-done | bytes 393248 | tf_op jit(solution)/shard_map/ppermute | solution.py:23
  404.8 27.3 %all-gather = f32[24,128,64]{2,0,1:T(8,128)S(1)} all-gather(f32[24,8,64]{2,0,1:T(8,128)S(1)} %copy.270), channel_id=2, replica_groups=mesh['runs'=2,'space'=16] {'space'}, dimensions={1}, use_global_device_ids=true | all-gather | bytes 835584 | tf_op jit(solution)/shard_map/all_gather | solution.py:219
  (224 shorter events, 81.2 us)
Async XLA Ops:
  6.5 3.1 copy-start.23
  6.5 3.8 copy-start.16
  6.5 3.9 copy-start.25
  6.5 5.9 %copy-start.20 = (f32[24,24]{1,0:T(8,128)S(1)}, f32[24,24]{1,0:T(8,128)}, u32[]{:S(2)}) copy-start(f32[24,24]{1,0:T(8,128)} %param.10) | copy-start | bytes 6916
  6.5 247.7 %all-reduce.4.cloned.1.call-start = ((), (), s32[]{:S(2)}) async-start(), calls=%async_computation | async-start | bytes 15335424 | tf_op jit(solution)/shard_map/psum | solution.py:172
  7.8 6.6 %collective-permute-start = (f32[24,2,16,128]{3,2,1,0:T(8,128)S(1)}, f32[24,2,16,128]{3,2,1,0:T(8,128)S(1)}, u32[]{:S(2)}, u32[]{:S(2)}) collective-permute-start(f32[24,2,16,128]{3,2,1,0:T(8,128)S(1)} %get-tuple-element.60), channel_id=1, source_target_pairs={{0,1},{1,2},{2,3},{3,4},{4,5},{5,6},{6,7},{7,8},{8,9},{9,10},{10,1... | collective-permute-start | bytes 1179656 | tf_op jit(solution)/shard_map/ppermute | solution.py:22
  9.6 8.2 %collective-permute-start.1 = (f32[24,2,16,128]{3,2,1,0:T(8,128)S(1)}, f32[24,2,16,128]{3,2,1,0:T(8,128)S(1)}, u32[]{:S(2)}, u32[]{:S(2)}) collective-permute-start(f32[24,2,16,128]{3,2,1,0:T(8,128)S(1)} %get-tuple-element.60), channel_id=1, source_target_pairs={{1,0},{2,1},{3,2},{4,3},{5,4},{6,5},{7,6},{8,7},{9,8},{10,9},{11,1... | collective-permute-start | bytes 1179656 | tf_op jit(solution)/shard_map/ppermute | solution.py:23
  18.9 1.7 copy-start
  21.6 4.8 %collective-permute-start.2 = (f32[24,2,16,128]{3,2,1,0:T(8,128)S(1)}, f32[24,2,16,128]{3,2,1,0:T(8,128)S(1)}, u32[]{:S(2)}, u32[]{:S(2)}) collective-permute-start(f32[24,2,16,128]{3,2,1,0:T(8,128)S(1)} %get-tuple-element.32), channel_id=1, source_target_pairs={{0,1},{1,2},{2,3},{3,4},{4,5},{5,6},{6,7},{7,8},{8,9},{9,10},{10,1... | collective-permute-start | bytes 1179656 | tf_op jit(solution)/shard_map/ppermute | solution.py:22
  21.6 9.5 %collective-permute-start.3 = (f32[24,2,16,128]{3,2,1,0:T(8,128)S(1)}, f32[24,2,16,128]{3,2,1,0:T(8,128)S(1)}, u32[]{:S(2)}, u32[]{:S(2)}) collective-permute-start(f32[24,2,16,128]{3,2,1,0:T(8,128)S(1)} %get-tuple-element.32), channel_id=1, source_target_pairs={{1,0},{2,1},{3,2},{4,3},{5,4},{6,5},{7,6},{8,7},{9,8},{10,9},{11,1... | collective-permute-start | bytes 1179656 | tf_op jit(solution)/shard_map/ppermute | solution.py:23
  34.3 16.4 %collective-permute-start.4 = (f32[24,2,16,128]{3,2,1,0:T(8,128)S(1)}, f32[24,2,16,128]{3,2,1,0:T(8,128)S(1)}, u32[]{:S(2)}, u32[]{:S(2)}) collective-permute-start(f32[24,2,16,128]{3,2,1,0:T(8,128)S(1)} %get-tuple-element.30), channel_id=1, source_target_pairs={{0,1},{1,2},{2,3},{3,4},{4,5},{5,6},{6,7},{7,8},{8,9},{9,10},{10,1... | collective-permute-start | bytes 1179656 | tf_op jit(solution)/shard_map/ppermute | solution.py:22
  34.4 20.7 %collective-permute-start.5 = (f32[24,2,16,128]{3,2,1,0:T(8,128)S(1)}, f32[24,2,16,128]{3,2,1,0:T(8,128)S(1)}, u32[]{:S(2)}, u32[]{:S(2)}) collective-permute-start(f32[24,2,16,128]{3,2,1,0:T(8,128)S(1)} %get-tuple-element.30), channel_id=1, source_target_pairs={{1,0},{2,1},{3,2},{4,3},{5,4},{6,5},{7,6},{8,7},{9,8},{10,9},{11,1... | collective-permute-start | bytes 1179656 | tf_op jit(solution)/shard_map/ppermute | solution.py:23
  58.3 4.8 %collective-permute-start.6 = (f32[24,2,16,128]{3,2,1,0:T(8,128)S(1)}, f32[24,2,16,128]{3,2,1,0:T(8,128)S(1)}, u32[]{:S(2)}, u32[]{:S(2)}) collective-permute-start(f32[24,2,16,128]{3,2,1,0:T(8,128)S(1)} %get-tuple-element.28), channel_id=1, source_target_pairs={{0,1},{1,2},{2,3},{3,4},{4,5},{5,6},{6,7},{7,8},{8,9},{9,10},{10,1... | collective-permute-start | bytes 1179656 | tf_op jit(solution)/shard_map/ppermute | solution.py:22
  58.4 9.8 %collective-permute-start.7 = (f32[24,2,16,128]{3,2,1,0:T(8,128)S(1)}, f32[24,2,16,128]{3,2,1,0:T(8,128)S(1)}, u32[]{:S(2)}, u32[]{:S(2)}) collective-permute-start(f32[24,2,16,128]{3,2,1,0:T(8,128)S(1)} %get-tuple-element.28), channel_id=1, source_target_pairs={{1,0},{2,1},{3,2},{4,3},{5,4},{6,5},{7,6},{8,7},{9,8},{10,9},{11,1... | collective-permute-start | bytes 1179656 | tf_op jit(solution)/shard_map/ppermute | solution.py:23
  78.3 4.7 %copy-start.21 = (f32[3,2]{0,1:T(2,128)S(1)}, f32[3,2]{0,1:T(2,128)}, u32[]{:S(2)}) copy-start(f32[3,2]{0,1:T(2,128)} %get-tuple-element.138) | copy-start | bytes 76
  78.3 4.7 %copy-start.22 = (f32[3,2]{0,1:T(2,128)S(1)}, f32[3,2]{0,1:T(2,128)}, u32[]{:S(2)}) copy-start(f32[3,2]{0,1:T(2,128)} %get-tuple-element.139) | copy-start | bytes 76
  80.1 5.3 %copy-start.15 = (f32[24,2,12,3]{0,1,3,2:T(2,128)S(1)}, f32[24,2,12,3]{0,1,3,2:T(2,128)}, u32[]{:S(2)}) copy-start(f32[24,2,12,3]{0,1,3,2:T(2,128)} %copy.230) | copy-start | bytes 20740
  80.1 5.3 %copy-start.19 = (pred[20,2,1,1]{0,1,3,2:T(4,128)(4,1)S(1)}, pred[20,2,1,1]{0,1,3,2:T(4,128)(4,1)}, u32[]{:S(2)}) copy-start(pred[20,2,1,1]{0,1,3,2:T(4,128)(4,1)} %get-tuple-element.141) | copy-start | bytes 124
  89.0 193.2 %collective-permute-start.8 = (f32[24,2,16,128]{3,2,1,0:T(8,128)S(1)}, f32[24,2,16,128]{3,2,1,0:T(8,128)}, u32[]{:S(2)}, u32[]{:S(2)}) collective-permute-start(f32[24,2,16,128]{3,2,1,0:T(8,128)S(1)} %get-tuple-element.61), channel_id=1, source_target_pairs={{0,1},{1,2},{2,3},{3,4},{4,5},{5,6},{6,7},{7,8},{8,9},{9,10},{10,1... | collective-permute-start | bytes 1179656 | tf_op jit(solution)/shard_map/ppermute | solution.py:22
  91.0 191.3 %collective-permute-start.9 = (f32[24,2,16,128]{3,2,1,0:T(8,128)S(1)}, f32[24,2,16,128]{3,2,1,0:T(8,128)}, u32[]{:S(2)}, u32[]{:S(2)}) collective-permute-start(f32[24,2,16,128]{3,2,1,0:T(8,128)S(1)} %get-tuple-element.61), channel_id=1, source_target_pairs={{1,0},{2,1},{3,2},{4,3},{5,4},{6,5},{7,6},{8,7},{9,8},{10,9},{11,1... | collective-permute-start | bytes 1179656 | tf_op jit(solution)/shard_map/ppermute | solution.py:23
  254.2 6.8 %copy-start.10 = (f32[24,6,12,68]{3,1,2,0:T(8,128)S(1)}, f32[24,6,12,68]{3,1,2,0:T(8,128)}, u32[]{:S(2)}) copy-start(f32[24,6,12,68]{3,1,2,0:T(8,128)} %get-tuple-element.10) | copy-start | bytes 1410052
  261.1 2.0 copy-start.9
  263.1 2.9 copy-start.12
  266.0 7.2 %copy-start.11 = (f32[24,20,12,6]{1,0,3,2:T(8,128)S(1)}, f32[24,20,12,6]{1,0,3,2:T(8,128)}, u32[]{:S(2)}) copy-start(f32[24,20,12,6]{1,0,3,2:T(8,128)} %get-tuple-element.6) | copy-start | bytes 414724
  278.9 1.4 copy-start.3
  286.7 8.7 %collective-permute-start.10 = (f32[24,2,16,128]{3,2,1,0:T(8,128)S(1)}, f32[24,2,16,128]{3,2,1,0:T(8,128)S(1)}, u32[]{:S(2)}, u32[]{:S(2)}) collective-permute-start(f32[24,2,16,128]{3,2,1,0:T(8,128)S(1)} %get-tuple-element.26), channel_id=1, source_target_pairs={{0,1},{1,2},{2,3},{3,4},{4,5},{5,6},{6,7},{7,8},{8,9},{9,10},{10,1... | collective-permute-start | bytes 1179656 | tf_op jit(solution)/shard_map/ppermute | solution.py:22
  290.7 10.0 %collective-permute-start.11 = (f32[24,2,16,128]{3,2,1,0:T(8,128)S(1)}, f32[24,2,16,128]{3,2,1,0:T(8,128)S(1)}, u32[]{:S(2)}, u32[]{:S(2)}) collective-permute-start(f32[24,2,16,128]{3,2,1,0:T(8,128)S(1)} %get-tuple-element.26), channel_id=1, source_target_pairs={{1,0},{2,1},{3,2},{4,3},{5,4},{6,5},{7,6},{8,7},{9,8},{10,9},{11,1... | collective-permute-start | bytes 1179656 | tf_op jit(solution)/shard_map/ppermute | solution.py:23
  303.1 6.8 %copy-start.14 = (f32[24,2,4,128]{3,0,2,1:T(8,128)S(1)}, f32[24,2,4,128]{3,0,2,1:T(8,128)}, u32[]{:S(2)}) copy-start(f32[24,2,4,128]{3,0,2,1:T(8,128)} %get-tuple-element.153) | copy-start | bytes 294916
  304.0 6.6 %collective-permute-start.12 = (f32[24,2,16,128]{3,2,1,0:T(8,128)S(1)}, f32[24,2,16,128]{3,2,1,0:T(8,128)S(1)}, u32[]{:S(2)}, u32[]{:S(2)}) collective-permute-start(f32[24,2,16,128]{3,2,1,0:T(8,128)S(1)} %get-tuple-element.24), channel_id=1, source_target_pairs={{0,1},{1,2},{2,3},{3,4},{4,5},{5,6},{6,7},{7,8},{8,9},{9,10},{10,1... | collective-permute-start | bytes 1179656 | tf_op jit(solution)/shard_map/ppermute | solution.py:22
  306.0 10.1 %collective-permute-start.13 = (f32[24,2,16,128]{3,2,1,0:T(8,128)S(1)}, f32[24,2,16,128]{3,2,1,0:T(8,128)S(1)}, u32[]{:S(2)}, u32[]{:S(2)}) collective-permute-start(f32[24,2,16,128]{3,2,1,0:T(8,128)S(1)} %get-tuple-element.24), channel_id=1, source_target_pairs={{1,0},{2,1},{3,2},{4,3},{5,4},{6,5},{7,6},{8,7},{9,8},{10,9},{11,1... | collective-permute-start | bytes 1179656 | tf_op jit(solution)/shard_map/ppermute | solution.py:23
  319.4 6.6 %collective-permute-start.14 = (f32[24,2,16,128]{3,2,1,0:T(8,128)S(1)}, f32[24,2,16,128]{3,2,1,0:T(8,128)S(1)}, u32[]{:S(2)}, u32[]{:S(2)}) collective-permute-start(f32[24,2,16,128]{3,2,1,0:T(8,128)S(1)} %get-tuple-element.22), channel_id=1, source_target_pairs={{0,1},{1,2},{2,3},{3,4},{4,5},{5,6},{6,7},{7,8},{8,9},{9,10},{10,1... | collective-permute-start | bytes 1179656 | tf_op jit(solution)/shard_map/ppermute | solution.py:22
  321.4 10.1 %collective-permute-start.15 = (f32[24,2,16,128]{3,2,1,0:T(8,128)S(1)}, f32[24,2,16,128]{3,2,1,0:T(8,128)S(1)}, u32[]{:S(2)}, u32[]{:S(2)}) collective-permute-start(f32[24,2,16,128]{3,2,1,0:T(8,128)S(1)} %get-tuple-element.22), channel_id=1, source_target_pairs={{1,0},{2,1},{3,2},{4,3},{5,4},{6,5},{7,6},{8,7},{9,8},{10,9},{11,1... | collective-permute-start | bytes 1179656 | tf_op jit(solution)/shard_map/ppermute | solution.py:23
  334.8 8.4 %collective-permute-start.16 = (f32[24,2,16,128]{3,2,1,0:T(8,128)S(1)}, f32[24,2,16,128]{3,2,1,0:T(8,128)S(1)}, u32[]{:S(2)}, u32[]{:S(2)}) collective-permute-start(f32[24,2,16,128]{3,2,1,0:T(8,128)S(1)} %fusion.104), channel_id=1, source_target_pairs={{0,1},{1,2},{2,3},{3,4},{4,5},{5,6},{6,7},{7,8},{8,9},{9,10},{10,1... | collective-permute-start | bytes 1179656 | tf_op jit(solution)/shard_map/ppermute | solution.py:22
  336.8 10.7 %collective-permute-start.17 = (f32[24,2,16,128]{3,2,1,0:T(8,128)S(1)}, f32[24,2,16,128]{3,2,1,0:T(8,128)S(1)}, u32[]{:S(2)}, u32[]{:S(2)}) collective-permute-start(f32[24,2,16,128]{3,2,1,0:T(8,128)S(1)} %fusion.104), channel_id=1, source_target_pairs={{1,0},{2,1},{3,2},{4,3},{5,4},{6,5},{7,6},{8,7},{9,8},{10,9},{11,1... | collective-permute-start | bytes 1179656 | tf_op jit(solution)/shard_map/ppermute | solution.py:23
  350.8 7.6 %collective-permute-start.18 = (f32[24,2,16,128]{3,2,1,0:T(8,128)S(1)}, f32[24,2,16,128]{3,2,1,0:T(8,128)S(1)}, u32[]{:S(2)}, u32[]{:S(2)}) collective-permute-start(f32[24,2,16,128]{3,2,1,0:T(8,128)S(1)} %get-tuple-element.20), channel_id=1, source_target_pairs={{0,1},{1,2},{2,3},{3,4},{4,5},{5,6},{6,7},{7,8},{8,9},{9,10},{10,1... | collective-permute-start | bytes 1179656 | tf_op jit(solution)/shard_map/ppermute | solution.py:22
  352.8 11.4 %collective-permute-start.19 = (f32[24,2,16,128]{3,2,1,0:T(8,128)S(1)}, f32[24,2,16,128]{3,2,1,0:T(8,128)S(1)}, u32[]{:S(2)}, u32[]{:S(2)}) collective-permute-start(f32[24,2,16,128]{3,2,1,0:T(8,128)S(1)} %get-tuple-element.20), channel_id=1, source_target_pairs={{1,0},{2,1},{3,2},{4,3},{5,4},{6,5},{7,6},{8,7},{9,8},{10,9},{11,1... | collective-permute-start | bytes 1179656 | tf_op jit(solution)/shard_map/ppermute | solution.py:23
  357.4 9.1 %copy-start.5 = (f32[24,2,2,128]{3,2,1,0:T(2,128)}, f32[24,2,2,128]{3,2,1,0:T(2,128)S(1)}, u32[]{:S(2)}) copy-start(f32[24,2,2,128]{3,2,1,0:T(2,128)S(1)} %get-tuple-element.127) | copy-start | bytes 147460
  357.4 9.1 %copy-start.7 = (f32[24,2,2,128]{3,2,1,0:T(2,128)}, f32[24,2,2,128]{3,2,1,0:T(2,128)S(1)}, u32[]{:S(2)}) copy-start(f32[24,2,2,128]{3,2,1,0:T(2,128)S(1)} %get-tuple-element.128) | copy-start | bytes 147460
  368.3 14.0 %collective-permute-start.20 = (f32[24,2,16,128]{3,2,1,0:T(8,128)S(1)}, f32[24,2,16,128]{3,2,1,0:T(8,128)}, u32[]{:S(2)}, u32[]{:S(2)}) collective-permute-start(f32[24,2,16,128]{3,2,1,0:T(8,128)S(1)} %get-tuple-element.18), channel_id=1, source_target_pairs={{0,1},{1,2},{2,3},{3,4},{4,5},{5,6},{6,7},{7,8},{8,9},{9,10},{10,1... | collective-permute-start | bytes 1179656 | tf_op jit(solution)/shard_map/ppermute | solution.py:22
  370.2 12.1 %collective-permute-start.21 = (f32[24,2,16,128]{3,2,1,0:T(8,128)S(1)}, f32[24,2,16,128]{3,2,1,0:T(8,128)}, u32[]{:S(2)}, u32[]{:S(2)}) collective-permute-start(f32[24,2,16,128]{3,2,1,0:T(8,128)S(1)} %get-tuple-element.18), channel_id=1, source_target_pairs={{1,0},{2,1},{3,2},{4,3},{5,4},{6,5},{7,6},{8,7},{9,8},{10,9},{11,1... | collective-permute-start | bytes 1179656 | tf_op jit(solution)/shard_map/ppermute | solution.py:23
  382.3 1.3 copy-start.6
  385.8 6.9 %copy-start.13 = (f32[24,2,4,128]{3,2,1,0:T(4,128)S(1)}, f32[24,2,4,128]{3,2,1,0:T(4,128)}, u32[]{:S(2)}) copy-start(f32[24,2,4,128]{3,2,1,0:T(4,128)} %get-tuple-element.121) | copy-start | bytes 294916
  386.8 7.8 %collective-permute-start.22 = (f32[24,2,16,128]{3,2,1,0:T(8,128)S(1)}, f32[24,2,16,128]{3,2,1,0:T(8,128)S(1)}, u32[]{:S(2)}, u32[]{:S(2)}) collective-permute-start(f32[24,2,16,128]{3,2,1,0:T(8,128)S(1)} %get-tuple-element.16), channel_id=1, source_target_pairs={{0,1},{1,2},{2,3},{3,4},{4,5},{5,6},{6,7},{7,8},{8,9},{9,10},{10,1... | collective-permute-start | bytes 1179656 | tf_op jit(solution)/shard_map/ppermute | solution.py:22
  389.9 10.1 %collective-permute-start.23 = (f32[24,2,16,128]{3,2,1,0:T(8,128)S(1)}, f32[24,2,16,128]{3,2,1,0:T(8,128)S(1)}, u32[]{:S(2)}, u32[]{:S(2)}) collective-permute-start(f32[24,2,16,128]{3,2,1,0:T(8,128)S(1)} %get-tuple-element.16), channel_id=1, source_target_pairs={{1,0},{2,1},{3,2},{4,3},{5,4},{6,5},{7,6},{8,7},{9,8},{10,9},{11,1... | collective-permute-start | bytes 1179656 | tf_op jit(solution)/shard_map/ppermute | solution.py:23
  392.7 7.2 %copy-start.1 = (f32[24,4,16,128]{3,2,1,0:T(8,128)S(1)}, f32[24,4,16,128]{3,2,1,0:T(8,128)}, u32[]{:S(2)}) copy-start(f32[24,4,16,128]{3,2,1,0:T(8,128)} %get-tuple-element.34) | copy-start | bytes 2359300
  400.6 1.7 copy-start.4
  403.8 28.3 %copy-start.24 = (s32[2]{0:T(128)S(1)}, s32[2]{0:T(128)}, u32[]{:S(2)}) copy-start(s32[2]{0:T(128)} %get-tuple-element.13) | copy-start | bytes 28
  432.1 1.7 copy-start.17
  (3 other events, 3.5 us)
Sparse Core Ops, SparseCore 0:
  89.2 165.0 all-reduce.3
where the time goes:
time: 450 us; the launch traced here: 442 us
  waiting for transfers between devices  214 us (48%)
  starting transfers between devices  68.6 us (15%)
  matrix products  59.8 us (13%)
  other arithmetic  41.2 us (9%)
  blocking collectives  27.3 us (6%)
  between operations  20.6 us (5%)
  local copies, waits for them, and re-layouts  10.2 us (2%)
    psum x1, waiting for transfers between devices, local(): lax.psum((rows_old, depth_old, ends_old, rows_new, depth_new, ends_new),...  158 us
    ppermute x12, waiting for transfers between devices, padded_2(): after = lax.ppermute(first, axis, down)  49.1 us
    ppermute x12, starting transfers between devices, padded_2(): after = lax.ppermute(first, axis, down)  48 us
    all_gather x1, blocking collectives, local(): arrived = lax.all_gather(restricted, 'space', axis=1, tiled=True)  27.3 us
    dot_general x18, matrix products, prolong(): jnp.einsum('ai,bj,ck,fijk->fabc', weights_across, weights_rows, weights_d...  24.7 us
    ppermute x12, starting transfers between devices, padded_2(): before = lax.ppermute(last, axis, up)  20.6 us
    dot_general x12, matrix products, tendency(): coupled = jnp.einsum('fg,gxyz->fxyz', mixing, stacked, precision=highest)  20.5 us
    dot_general x6, matrix products, into_window(): return jnp.einsum('wk,fkyz->fwyz', select, source, precision=highest)  13.1 us
  transfers between devices with their start and end apart: 25, of which 17 were waited for; matrix products, arithmetic and copies ran while one was open for 10% of the time, Pallas kernels for 0%

commit v1 on v0

v1 whole, which is shorter than its diff:
```python
import jax
import jax.numpy as jnp
from jax import lax
from jax.experimental import pallas as pl
from jax.experimental.pallas import tpu as pltpu
from jax.sharding import PartitionSpec as P

coarse_step = 0.25
damping = 0.2
fractions = (0.0, 0.5, 0.5, 1.0)
f32, bf16 = jnp.float32, jnp.bfloat16


def split_dot(x, m):
    hi = x.astype(bf16)
    lo = (x - hi.astype(f32)).astype(bf16)
    return jnp.dot(hi, m, preferred_element_type=f32) + jnp.dot(lo, m, preferred_element_type=f32)


def hat(j):
    location = 2 * j + 3
    low = location // 4
    return low, 1.0 - (location % 4) / 4.0, (location % 4) / 4.0


def kernel(n, off_ref, mix_ref, diff_ref, lev_ref, zsel_ref, exp_ref, expx_ref, mean_ref, place_ref, out_ref,
           u_buf, l_buf, r_buf, start, acc, weights, pay, gath, gy, gz, gx, means, landed,
           halo_send, halo_recv, all_send, all_recv):
    planes, rows, fields, depth = lev_ref.shape[1:]
    total = planes * n
    half_x, half_y, half_z = total // 2, rows // 2, depth // 2
    win_y = half_y + 4
    me = lax.axis_index("space")
    right, left = lax.rem(me + 1, n), lax.rem(me + n - 1, n)
    p, q = off_ref[0], off_ref[1]

    barrier = pltpu.get_barrier_semaphore()

    @pl.loop(1, n)
    def _(k):
        pl.semaphore_signal(barrier, inc=1, device_id={"space": lax.rem(me + k, n)}, device_id_type=pl.DeviceIdType.MESH)

    pl.semaphore_wait(barrier, n - 1)

    def send_all(src, dst, kind):
        @pl.loop(1, n)
        def _(k):
            pltpu.make_async_remote_copy(
                src_ref=src, dst_ref=dst, send_sem=all_send.at[kind, k], recv_sem=all_recv.at[kind, k],
                device_id={"space": lax.rem(me + k, n)}, device_id_type=pl.DeviceIdType.MESH).start()

    def wait_all(src, dst, kind):
        @pl.loop(1, n)
        def _(k):
            pltpu.make_async_remote_copy(
                src_ref=src, dst_ref=dst, send_sem=all_send.at[kind, k], recv_sem=all_recv.at[kind, k],
                device_id={"space": lax.rem(me + k, n)}, device_id_type=pl.DeviceIdType.MESH).wait()

    def halo(slot):
        copies = []
        for side, target, dst in ((0, right, l_buf), (1, left, r_buf)):
            copies.append(pltpu.make_async_remote_copy(
                src_ref=u_buf.at[slot, :, pl.ds(2, rows)], dst_ref=dst.at[slot],
                send_sem=halo_send.at[slot, side], recv_sem=halo_recv.at[slot, side],
                device_id={"space": target}, device_id_type=pl.DeviceIdType.MESH))
        return copies

    def pack_window(load, kind):
        for x in range(planes):
            picked = [load(x, lax.rem(q + rows - 2 + a, rows)) for a in range(win_y)]
            got = split_dot(jnp.concatenate(picked, axis=0), zsel_ref[...])
            for t in range(win_y // 2):
                even = got[2 * t * fields:(2 * t + 1) * fields, :depth]
                odd = got[(2 * t + 1) * fields:(2 * t + 2) * fields, :depth]
                pay[kind, x, t] = even + pltpu.roll(odd, half_z, 1)
            extra = got[:fields, depth:]
            for a in range(1, win_y):
                extra = extra + pltpu.roll(got[a * fields:(a + 1) * fields, depth:], 4 * a, 1)
            pay[kind, x, win_y // 2] = extra

    lanes = lax.broadcasted_iota(jnp.int32, (fields, depth), 1)
    stage = [0]

    def set_weights(spacing):
        column = lax.broadcasted_iota(jnp.int32, (fields, 4 * fields), 1)
        row = lax.broadcasted_iota(jnp.int32, (fields, 4 * fields), 0)
        c = damping / (16.0 * spacing)
        square = 12.0 * spacing * spacing
        diff = diff_ref[:, :1]
        diagonal = diff * (-90.0 / square) - 18.0 * c
        m = mix_ref[...]
        m = jnp.where(column < 3 * fields, m * (1.0 / (12.0 * spacing)),
                      m + jnp.where(column - 3 * fields == row, diagonal, 0.0))
        hi = m.astype(bf16).astype(f32)
        lo = m - hi
        weights[...] = jnp.concatenate(
            [jnp.concatenate([hi, hi], axis=1), jnp.concatenate([lo, jnp.zeros_like(lo)], axis=1)], axis=0).astype(bf16)
        dif = diff_ref[...]
        return dif * (16.0 / square) + 4.0 * c, dif * (-1.0 / square) - c

    def run_stage(section, step, near, far, t, last_store):
        slot = stage[0] % 2
        following = 1 - slot
        copies = halo(slot)
        for copy in copies:
            copy.start()
        if stage[0] > 0:
            for copy in halo(following):
                copy.wait_send()
        for copy in copies:
            copy.wait_recv()
        if t is not None:
            for edge, buf in ((0, l_buf), (n - 1, r_buf)):
                @pl.when(me == edge)
                def _(buf=buf):
                    @pl.loop(0, rows)
                    def _(y):
                        for x in range(planes):
                            buf[slot, x, y] = (1.0 - t) * gx[0, x, y] + t * gx[1, x, y]

        def body(y, carry):
            line = [l_buf[slot, 0, y], l_buf[slot, 1, y], u_buf[slot, 0, y + 2], u_buf[slot, 1, y + 2],
                    r_buf[slot, 0, y], r_buf[slot, 1, y]]
            stacks, even = [], []
            for x in range(planes):
                c = line[x + 2]
                terms = [(line[x], line[x + 1], line[x + 3], line[x + 4]),
                         tuple(u_buf[slot, x, y + 2 + k] for k in (-2, -1, 1, 2))]
                if t is None:
                    lo2 = lo1 = hi1 = hi2 = c
                else:
                    g = (1.0 - t) * gz[0, x, y] + t * gz[1, x, y]
                    lo2 = jnp.where(lanes >= depth - 2, g, c)
                    lo1 = jnp.where(lanes == depth - 1, g, c)
                    hi1 = jnp.where(lanes == 0, g, c)
                    hi2 = jnp.where(lanes <= 1, g, c)
                terms.append((pltpu.roll(lo2, 2, 1), pltpu.roll(lo1, 1, 1),
                              pltpu.roll(hi1, depth - 1, 1), pltpu.roll(hi2, depth - 2, 1)))
                stacks.append(jnp.concatenate(
                    [8.0 * (p1 - m1) - (p2 - m2) for m2, m1, p1, p2 in terms] + [c], axis=0))
                one = sum(m1 + p1 for _, m1, p1, _ in terms)
                two = sum(m2 + p2 for m2, _, _, p2 in terms)
                even.append(near * one + far * two)
            wide = jnp.concatenate(stacks, axis=1)
            hi = wide.astype(bf16)
            lo = (wide - hi.astype(f32)).astype(bf16)
            got = jnp.dot(weights[...], jnp.concatenate([hi, lo], axis=0), preferred_element_type=f32)
            got = got[:fields] + got[fields:]
            for x in range(planes):
                rate = got[:, x * depth:(x + 1) * depth] + even[x]
                if section == 0:
                    acc[x, y] = start[x, y] + (step / 6.0) * rate
                elif section < 3:
                    acc[x, y] = acc[x, y] + (step / 3.0) * rate
                if section < 3:
                    u_buf[following, x, y + 2] = start[x, y] + (step if section == 2 else 0.5 * step) * rate
                else:
                    last_store(x, y, acc[x, y] + (step / 6.0) * rate, following)
            return carry

        lax.fori_loop(0, rows, body, 0, unroll=2)
        stage[0] += 1

    def wrap_rows():
        slot = stage[0] % 2
        for x in range(planes):
            for k in range(2):
                u_buf[slot, x, k] = u_buf[slot, x, rows + k]
                u_buf[slot, x, rows + 2 + k] = u_buf[slot, x, 2 + k]

    def ghost_rows(t):
        slot = stage[0] % 2
        for x in range(planes):
            for k in range(4):
                row = k if k < 2 else rows + k
                u_buf[slot, x, row] = (1.0 - t) * gy[0, x, k] + t * gy[1, x, k]

    near, far = set_weights(1.0)

    @pl.loop(0, rows)
    def _(y):
        for x in range(planes):
            start[x, y] = lev_ref[0, x, y]
            u_buf[0, x, y + 2] = lev_ref[0, x, y]

    pack_window(lambda x, y: lev_ref[0, x, y], 0)
    gath[0, me] = pay[0]
    send_all(pay.at[0], gath.at[0, me], 0)

    def coarse_store(x, y, value, following):
        start[x, y] = value

    for section in range(4):
        wrap_rows()
        run_stage(section, coarse_step, near, far, None, coarse_store)

    pack_window(lambda x, y: start[x, y], 1)
    gath[1, me] = pay[1]
    send_all(pay.at[1], gath.at[1, me], 1)

    near, far = set_weights(0.5)

    @pl.loop(0, rows)
    def _(y):
        for x in range(planes):
            out_ref[0, x, y] = start[x, y]
            start[x, y] = lev_ref[1, x, y]
            u_buf[stage[0] % 2, x, y + 2] = lev_ref[1, x, y]

    wait_all(pay.at[0], gath.at[0, me], 0)
    wait_all(pay.at[1], gath.at[1, me], 1)

    def window_rows(t, first, w0, w1, which):
        g0 = lax.rem(p + total - 2 + first, total)
        g1 = lax.rem(p + total - 1 + first, total)
        tiles = [w0 * gath[t, g0 // planes, g0 % planes, k] + w1 * gath[t, g1 // planes, g1 % planes, k]
                 for k in range(win_y // 2 + 1)]
        main = split_dot(jnp.concatenate(tiles[:-1], axis=0), exp_ref[...])
        turned = [tiles[-1]] + [pltpu.roll(tiles[-1], depth - 4 * a, 1) for a in range(1, win_y)]
        extra = split_dot(jnp.concatenate(turned, axis=0), expx_ref[...])
        found = []
        for part in which:
            found.append([main[(a // 2) * fields:(a // 2 + 1) * fields,
                               (2 * part + a % 2) * depth:(2 * part + a % 2 + 1) * depth]
                          + extra[a * fields:(a + 1) * fields, part * depth:(part + 1) * depth] for a in range(win_y)])
        return found

    def mix_rows(lines, j):
        low, w0, w1 = hat(j)
        return w0 * lines[low] + w1 * lines[low + 1]

    @pl.loop(0, 2)
    def _(t):
        for x in range(planes):
            shift, w0, w1 = hat(x + 2)
            inner, outer = window_rows(t, me * (planes // 2) + shift, w0, w1, (0, 1))
            for k in range(4):
                gy[t, x, k] = mix_rows(inner, k if k < 2 else rows + k)
            for y in range(rows):
                gz[t, x, y] = mix_rows(outer, y + 2)
        for edge, base in ((0, 0), (n - 1, total + 2)):
            @pl.when(me == edge)
            def _(base=base):
                for x in range(2):
                    low, w0, w1 = hat(base + x)
                    inner, = window_rows(t, low, w0, w1, (0,))
                    for y in range(rows):
                        gx[t, x, y] = mix_rows(inner, y + 2)

    def fine_store(x, y, value, following):
        start[x, y] = value
        u_buf[following, x, y + 2] = value

    for substep in range(2):
        for section in range(4):
            t = 0.5 * (substep + fractions[section])
            ghost_rows(t)
            run_stage(section, 0.5 * coarse_step, near, far, t, fine_store)
    for copy in halo(1 - stage[0] % 2):
        copy.wait_send()

    folded = []
    for y in range(half_y):
        folded.append(start[0, 2 * y] + start[0, 2 * y + 1] + start[1, 2 * y] + start[1, 2 * y + 1])
    got = split_dot(jnp.concatenate(folded, axis=0), mean_ref[...])
    for t in range(half_y // 2):
        means[t] = (got[2 * t * fields:(2 * t + 1) * fields]
                    + pltpu.roll(got[(2 * t + 1) * fields:(2 * t + 2) * fields], half_z, 1))
        landed[me, t] = means[t]
    send_all(means, landed.at[me], 2)

    @pl.loop(0, rows)
    def _(y):
        for x in range(planes):
            out_ref[1, x, y] = start[x, y]

    wait_all(means, landed.at[me], 2)
    distance = lax.rem(lanes - off_ref[2] + depth, depth)
    for x in range(planes):
        relative = lax.rem(me * planes + x - p + total, total)
        source = lax.rem(relative, half_x)
        for k in range(half_y // 2):
            tile = landed[source, k]
            placed = split_dot(tile, place_ref[...])
            for parity in range(2):
                acc[0, 2 * k + parity] = placed[:, parity * depth:(parity + 1) * depth]
        for y in range(rows):
            row = lax.rem(y - q + rows, rows)
            value = acc[0, lax.rem(row, half_y)]
            limit = jnp.where(relative < half_x, jnp.where(row < half_y, half_z, 0), 0)
            out_ref[0, x, y] = jnp.where(distance < limit, value, out_ref[0, x, y])


def hats(fine, window):
    return jnp.maximum(0.0, 1.0 - jnp.abs(0.5 * fine.astype(f32) + 0.75 - window.astype(f32)))


def local(n, levels, region_offset, advect, coupling, diffusion):
    count, fields, planes, rows, depth = levels.shape
    half = depth // 2
    total = planes * n
    win_tiles = (rows // 2 + 4) // 2 + 1
    symmetric = 0.5 * (advect + jnp.swapaxes(advect, 1, 2))
    mixing = jnp.concatenate([symmetric[0], symmetric[1], symmetric[2], coupling], axis=1)
    spread = jnp.broadcast_to(diffusion[:, None], (fields, depth))
    swapped = jnp.transpose(levels, (0, 2, 3, 1, 4))
    r = region_offset[2]
    z = jnp.arange(depth, dtype=jnp.int32)[:, None]
    lane = jnp.arange(depth, dtype=jnp.int32)[None, :]
    zsel = jnp.concatenate([
        (lane < half) & (z == jnp.mod(r - 2 + lane, depth)),
        (lane < 4) & (z == jnp.mod(r - 2 + half + lane, depth))], axis=1).astype(bf16)
    outer = jnp.where(lane >= depth - 2, lane - (depth - 2), depth + 2 + lane)
    has = ((lane >= depth - 2) | (lane < 2)).astype(f32)
    parts = []
    for fine, mask in ((lane + 2, 1.0), (outer, has)):
        parts += [jnp.where(z < half, hats(fine, z), 0.0) * mask, jnp.where(z >= half, hats(fine, z - half), 0.0) * mask]
    expand = jnp.concatenate(parts, axis=1).astype(bf16)
    expandx = jnp.concatenate(
        [jnp.where(z < 4, hats(fine, z + half), 0.0) * mask for fine, mask in ((lane + 2, 1.0), (outer, has))],
        axis=1).astype(bf16)
    mean = ((z // 2 == lane) * 0.125).astype(bf16)
    target = jnp.mod(lane - r, depth)
    place = jnp.concatenate([(z == target) & (target < half), (z == target + half) & (target < half)], axis=1).astype(bf16)
    block = (planes, rows, fields, depth)
    vmem = pl.BlockSpec(memory_space=pltpu.VMEM)
    out = pl.pallas_call(
        lambda *refs: kernel(n, *refs),
        out_shape=jax.ShapeDtypeStruct(swapped.shape, f32),
        in_specs=[pl.BlockSpec(memory_space=pltpu.SMEM)] + [vmem] * 8,
        out_specs=vmem,
        scratch_shapes=[
            pltpu.VMEM((2, planes, rows + 4, fields, depth), f32),
            pltpu.VMEM((2,) + block, f32),
            pltpu.VMEM((2,) + block, f32),
            pltpu.VMEM(block, f32),
            pltpu.VMEM(block, f32),
            pltpu.VMEM((2 * fields, 8 * fields), bf16),
            pltpu.VMEM((2, planes, win_tiles, fields, depth), f32),
            pltpu.VMEM((2, n, planes, win_tiles, fields, depth), f32),
            pltpu.VMEM((2, planes, 4, fields, depth), f32),
            pltpu.VMEM((2,) + block, f32),
            pltpu.VMEM((2,) + block, f32),
            pltpu.VMEM((rows // 4, fields, depth), f32),
            pltpu.VMEM((n, rows // 4, fields, depth), f32),
            pltpu.SemaphoreType.DMA((2, 2)),
            pltpu.SemaphoreType.DMA((2, 2)),
            pltpu.SemaphoreType.DMA((3, n)),
            pltpu.SemaphoreType.DMA((3, n)),
        ],
        compiler_params=pltpu.CompilerParams(
            collective_id=0, has_side_effects=True, vmem_limit_bytes=48 * 1024 * 1024),
    )(region_offset, mixing, spread, swapped, zsel, expand, expandx, mean, place)
    return jnp.transpose(out, (0, 3, 1, 2, 4))


def solution(mesh):
    n = mesh.shape["space"]
    return jax.shard_map(
        lambda *args: local(n, *args),
        mesh=mesh,
        in_specs=(P("runs", None, "space", None, None), P("runs"), P(), P(), P()),
        out_specs=P("runs", None, "space", None, None),
        check_vma=False,
    )
```

time: 450 us -> 277 us (0.62); the launches traced: 442 us -> 276 us
  Pallas kernels: 0 us -> 266 us
  waiting for transfers between devices: 214 us -> 0 us
  starting transfers between devices: 68.6 us -> 0 us
  matrix products: 59.8 us -> 0 us
  other arithmetic: 41.2 us -> 3.32 us
  blocking collectives: 27.3 us -> 0 us
  between operations: 20.6 us -> 1.45 us
  local copies, waits for them, and re-layouts: 10.2 us -> 5.03 us
    pallas_call x0 -> x1, Pallas kernels: none -> 266 us  [local(): pl.pallas_call(lambda *refs: kernel(n, *refs), out_shape=jax.ShapeDtypeSt...]
    psum x1 -> x0, waiting for transfers between devices: 158 us -> none  [local(): lax.psum((rows_old, depth_old, ends_old, rows_new, depth_new, ends_new),...]
    ppermute x24 -> x0, starting transfers between devices: 68.6 us -> none  [the longest x12 48 us: padded_2(): after = lax.ppermute(first, axis, down)]
    dot_general x37 -> x0, matrix products: 59.8 us -> none  [the longest x18 24.7 us: prolong(): jnp.einsum('ai,bj,ck,fijk->fabc', weights_across, weights_rows, weights_d...]
    ppermute x24 -> x0, waiting for transfers between devices: 56.8 us -> none  [the longest x12 49.1 us: padded_2(): after = lax.ppermute(first, axis, down)]
    all_gather x1 -> x0, blocking collectives: 27.3 us -> none  [local(): arrived = lax.all_gather(restricted, 'space', axis=1, tiled=True)]
    add x23 -> x1, other arithmetic: 12.7 us -> 0.01 us  [hats(): 0.5 * fine.astype(f32) + 0.75 - window.astype(f32)]
    div x24 -> x0, other arithmetic: 12.6 us -> none  [the longest x23 12.6 us: stencil_terms(): (shifted[0] - 8.0 * shifted[1] + 8.0 * shifted[3] - shifted[4]) / (12.0 *...]
  transfers between devices with their start and end apart: 25 -> 0, of which waited for: 17 -> 0; matrix products, arithmetic and copies ran while one was open for 10% -> 0% of each run, Pallas kernels for 0% -> 0%
where the time goes in v1:
time: 277 us; the launch traced here: 276 us
  Pallas kernels  266 us (96%)
  local copies, waits for them, and re-layouts  5.03 us (2%)
  other arithmetic  3.32 us (1%)
    pallas_call x1, Pallas kernels, local(): pl.pallas_call(lambda *refs: kernel(n, *refs), out_shape=jax.ShapeDtypeSt...  266 us

profile of v1, /device:TPU:13, one launch (start us, length us, event | category | flops | bytes accessed | tf_op | source)
XLA Modules:
  0.0 275.6 jit_solution(6239094617284587567)
XLA Ops:
  0.0 0.0 copy-start.1
  0.0 1.3 slice.15
  2.7 0.7 broadcast_compare_fusion
  3.4 0.7 and_select_fusion
  4.1 0.7 broadcast_in_dim.48.refs_2_
  4.9 0.1 select_convert_fusion.refs_7_
  5.0 0.8 copy.6
  5.8 0.8 fusion.4
  6.6 0.8 pad_maximum_fusion.2.refs_1_
  7.4 0.2 select_convert_fusion.1
  7.6 0.0 copy-done.1
  7.6 0.5 copy.10
  8.1 0.0 copy-start
  8.1 0.6 copy-done
  8.8 265.8 %shard_map.55 = f32[2,2,16,24,128]{4,3,2,1,0:T(8,128)S(1)} custom-call(s32[3]{0:T(128)S(1)} %copy-done, f32[24,96]{1,0:T(8,128)S(1)} %pad_maximum_fusion.2.refs_1_, f32[24,128]{1,0:T(8,128)S(1)} %broadcast_in_dim.48.refs_2_, f32[2,2,16,24,128]{4,3,2,1,0:T(8,128)S(1)} %bitcast.16, bf16[128,256]{1,0:T(8,128)(2,1)S(1)} %add_convert_fusion.refs_4_, ...), custom_call_target="tpu_custom_call" | custom-call | tf_op jit(solution)/shard_map/pallas_call | solution.py:327
  274.6 1.0 copy.8
  (16 shorter events, 0.2 us)
Async XLA Ops:
  0.0 7.6 %copy-start.1 = (f32[2,24,2,16,128]{4,3,2,1,0:T(8,128)S(1)}, f32[2,24,2,16,128]{4,3,2,1,0:T(8,128)}, u32[]{:S(2)}) copy-start(f32[2,24,2,16,128]{4,3,2,1,0:T(8,128)} %param.5) | copy-start | bytes 2359300
  8.1 0.7 copy-start

commit v2 on v1

--- a/solution.py
+++ b/solution.py
@@ -24,7 +24,7 @@
 
 
 def kernel(n, off_ref, mix_ref, diff_ref, lev_ref, zsel_ref, exp_ref, expx_ref, mean_ref, place_ref, out_ref,
-           u_buf, l_buf, r_buf, start, acc, weights, pay, gath, gy, gz, gx, means, landed,
+           u_buf, l_buf, r_buf, start, acc, part, weights, weights_x, pay, gath_old, gath_new, gy, gz, gx, sums, landed,
            halo_send, halo_recv, all_send, all_recv):
     planes, rows, fields, depth = lev_ref.shape[1:]
     total = planes * n
@@ -42,19 +42,38 @@
 
     pl.semaphore_wait(barrier, n - 1)
 
-    def send_all(src, dst, kind):
-        @pl.loop(1, n)
+    core = lax.rem(me, 2)
+    pair = me // 2
+    across = me + 2 - 4 * lax.rem(pair, 2)
+    groups = n // 4
+    first = pair - lax.rem(pair, 2)
+
+    def remote(src, dst, kind, k, target):
+        return pltpu.make_async_remote_copy(
+            src_ref=src, dst_ref=dst, send_sem=all_send.at[kind, k], recv_sem=all_recv.at[kind, k],
+            device_id={"space": target}, device_id_type=pl.DeviceIdType.MESH)
+
+    def gather_start(dst, own, kind):
+        remote(own, dst.at[core, pair], kind, 0, across).start()
+
+    def gather_middle(dst, own, kind):
+        remote(own, dst.at[core, pair], kind, 0, across).wait()
+
+        @pl.loop(1, groups)
         def _(k):
-            pltpu.make_async_remote_copy(
-                src_ref=src, dst_ref=dst, send_sem=all_send.at[kind, k], recv_sem=all_recv.at[kind, k],
-                device_id={"space": lax.rem(me + k, n)}, device_id_type=pl.DeviceIdType.MESH).start()
-
-    def wait_all(src, dst, kind):
-        @pl.loop(1, n)
+            block = dst.at[core, pl.ds(first, 2)]
+            remote(block, block, kind, k, lax.rem(me + 4 * k, n)).start()
+
+    def gather_last(dst, kind):
+        @pl.loop(1, groups)
         def _(k):
-            pltpu.make_async_remote_copy(
-                src_ref=src, dst_ref=dst, send_sem=all_send.at[kind, k], recv_sem=all_recv.at[kind, k],
-                device_id={"space": lax.rem(me + k, n)}, device_id_type=pl.DeviceIdType.MESH).wait()
+            block = dst.at[core, pl.ds(first, 2)]
+            remote(block, block, kind, k, lax.rem(me + 4 * k, n)).wait()
+
+        remote(dst.at[core], dst.at[core], kind, groups, me + 1 - 2 * core).start()
+
+    def gather_end(dst, kind):
+        remote(dst.at[core], dst.at[core], kind, groups, me + 1 - 2 * core).wait()
 
     def halo(slot):
         copies = []
@@ -77,6 +96,11 @@
             for a in range(1, win_y):
                 extra = extra + pltpu.roll(got[a * fields:(a + 1) * fields, depth:], 4 * a, 1)
             pay[kind, x, win_y // 2] = extra
+
+    def blend(load, t):
+        if t in (0.0, 1.0):
+            return load(int(t))
+        return (1.0 - t) * load(0) + t * load(1)
 
     lanes = lax.broadcasted_iota(jnp.int32, (fields, depth), 1)
     stage = [0]
@@ -93,8 +117,10 @@
                       m + jnp.where(column - 3 * fields == row, diagonal, 0.0))
         hi = m.astype(bf16).astype(f32)
         lo = m - hi
-        weights[...] = jnp.concatenate(
-            [jnp.concatenate([hi, hi], axis=1), jnp.concatenate([lo, jnp.zeros_like(lo)], axis=1)], axis=0).astype(bf16)
+        for ref, cut in ((weights_x, slice(0, fields)), (weights, slice(fields, 4 * fields))):
+            h, l = hi[:, cut], lo[:, cut]
+            ref[...] = jnp.concatenate(
+                [jnp.concatenate([h, h], axis=1), jnp.concatenate([l, jnp.zeros_like(l)], axis=1)], axis=0).astype(bf16)
         dif = diff_ref[...]
         return dif * (16.0 / square) + 4.0 * c, dif * (-1.0 / square) - c
 
@@ -107,6 +133,39 @@
         if stage[0] > 0:
             for copy in halo(following):
                 copy.wait_send()
+        def product(stacks, factor):
+            wide = jnp.concatenate(stacks, axis=1)
+            hi = wide.astype(bf16).astype(f32)
+            both = jnp.concatenate([hi, wide - hi], axis=0).astype(bf16)
+            got = jnp.dot(factor[...], both, preferred_element_type=f32)
+            return got[:fields] + got[fields:]
+
+        def gradient(m2, m1, p1, p2):
+            return 8.0 * (p1 - m1) - (p2 - m2)
+
+        def before(y, carry):
+            stacks, even = [], []
+            for x in range(planes):
+                c = u_buf[slot, x, y + 2]
+                terms = [tuple(u_buf[slot, x, y + 2 + k] for k in (-2, -1, 1, 2))]
+                if t is None:
+                    lo2 = lo1 = hi1 = hi2 = c
+                else:
+                    g = blend(lambda i: gz[i, x, y], t)
+                    lo2 = jnp.where(lanes >= depth - 2, g, c)
+                    lo1 = jnp.where(lanes == depth - 1, g, c)
+                    hi1 = jnp.where(lanes == 0, g, c)
+                    hi2 = jnp.where(lanes <= 1, g, c)
+                terms.append((pltpu.roll(lo2, 2, 1), pltpu.roll(lo1, 1, 1),
+                              pltpu.roll(hi1, depth - 1, 1), pltpu.roll(hi2, depth - 2, 1)))
+                stacks.append(jnp.concatenate([gradient(*term) for term in terms] + [c], axis=0))
+                even.append(near * sum(m1 + p1 for _, m1, p1, _ in terms) + far * sum(m2 + p2 for m2, _, _, p2 in terms))
+            got = product(stacks, weights)
+            for x in range(planes):
+                part[x, y] = got[:, x * depth:(x + 1) * depth] + even[x]
+            return carry
+
+        lax.fori_loop(0, rows, before, 0, unroll=4)
         for copy in copies:
             copy.wait_recv()
         if t is not None:
@@ -116,36 +175,17 @@
                     @pl.loop(0, rows)
                     def _(y):
                         for x in range(planes):
-                            buf[slot, x, y] = (1.0 - t) * gx[0, x, y] + t * gx[1, x, y]
+                            buf[slot, x, y] = blend(lambda i: gx[i, x, y], t)
 
         def body(y, carry):
             line = [l_buf[slot, 0, y], l_buf[slot, 1, y], u_buf[slot, 0, y + 2], u_buf[slot, 1, y + 2],
                     r_buf[slot, 0, y], r_buf[slot, 1, y]]
             stacks, even = [], []
             for x in range(planes):
-                c = line[x + 2]
-                terms = [(line[x], line[x + 1], line[x + 3], line[x + 4]),
-                         tuple(u_buf[slot, x, y + 2 + k] for k in (-2, -1, 1, 2))]
-                if t is None:
-                    lo2 = lo1 = hi1 = hi2 = c
-                else:
-                    g = (1.0 - t) * gz[0, x, y] + t * gz[1, x, y]
-                    lo2 = jnp.where(lanes >= depth - 2, g, c)
-                    lo1 = jnp.where(lanes == depth - 1, g, c)
-                    hi1 = jnp.where(lanes == 0, g, c)
-                    hi2 = jnp.where(lanes <= 1, g, c)
-                terms.append((pltpu.roll(lo2, 2, 1), pltpu.roll(lo1, 1, 1),
-                              pltpu.roll(hi1, depth - 1, 1), pltpu.roll(hi2, depth - 2, 1)))
-                stacks.append(jnp.concatenate(
-                    [8.0 * (p1 - m1) - (p2 - m2) for m2, m1, p1, p2 in terms] + [c], axis=0))
-                one = sum(m1 + p1 for _, m1, p1, _ in terms)
-                two = sum(m2 + p2 for m2, _, _, p2 in terms)
-                even.append(near * one + far * two)
-            wide = jnp.concatenate(stacks, axis=1)
-            hi = wide.astype(bf16)
-            lo = (wide - hi.astype(f32)).astype(bf16)
-            got = jnp.dot(weights[...], jnp.concatenate([hi, lo], axis=0), preferred_element_type=f32)
-            got = got[:fields] + got[fields:]
+                m2, m1, p1, p2 = line[x], line[x + 1], line[x + 3], line[x + 4]
+                stacks.append(gradient(m2, m1, p1, p2))
+                even.append(part[x, y] + near * (m1 + p1) + far * (m2 + p2))
+            got = product(stacks, weights_x)
             for x in range(planes):
                 rate = got[:, x * depth:(x + 1) * depth] + even[x]
                 if section == 0:
@@ -158,7 +198,7 @@
                     last_store(x, y, acc[x, y] + (step / 6.0) * rate, following)
             return carry
 
-        lax.fori_loop(0, rows, body, 0, unroll=2)
+        lax.fori_loop(0, rows, body, 0, unroll=4)
         stage[0] += 1
 
     def wrap_rows():
@@ -173,7 +213,7 @@
         for x in range(planes):
             for k in range(4):
                 row = k if k < 2 else rows + k
-                u_buf[slot, x, row] = (1.0 - t) * gy[0, x, k] + t * gy[1, x, k]
+                u_buf[slot, x, row] = blend(lambda i: gy[i, x, k], t)
 
     near, far = set_weights(1.0)
 
@@ -184,8 +224,8 @@
             u_buf[0, x, y + 2] = lev_ref[0, x, y]
 
     pack_window(lambda x, y: lev_ref[0, x, y], 0)
-    gath[0, me] = pay[0]
-    send_all(pay.at[0], gath.at[0, me], 0)
+    gather_start(gath_old, pay.at[0], 0)
+    gath_old[core, pair] = pay[0]
 
     def coarse_store(x, y, value, following):
         start[x, y] = value
@@ -193,10 +233,14 @@
     for section in range(4):
         wrap_rows()
         run_stage(section, coarse_step, near, far, None, coarse_store)
+        if section == 0:
+            gather_middle(gath_old, pay.at[0], 0)
+        elif section == 2:
+            gather_last(gath_old, 0)
 
     pack_window(lambda x, y: start[x, y], 1)
-    gath[1, me] = pay[1]
-    send_all(pay.at[1], gath.at[1, me], 1)
+    gather_start(gath_new, pay.at[1], 1)
+    gath_new[core, pair] = pay[1]
 
     near, far = set_weights(0.5)
 
@@ -207,13 +251,16 @@
             start[x, y] = lev_ref[1, x, y]
             u_buf[stage[0] % 2, x, y + 2] = lev_ref[1, x, y]
 
-    wait_all(pay.at[0], gath.at[0, me], 0)
-    wait_all(pay.at[1], gath.at[1, me], 1)
+    gather_end(gath_old, 0)
+
+    def held(t, g, k):
+        d = g // planes
+        return (gath_old, gath_new)[t][lax.rem(d, 2), d // 2, lax.rem(g, planes), k]
 
     def window_rows(t, first, w0, w1, which):
         g0 = lax.rem(p + total - 2 + first, total)
         g1 = lax.rem(p + total - 1 + first, total)
-        tiles = [w0 * gath[t, g0 // planes, g0 % planes, k] + w1 * gath[t, g1 // planes, g1 % planes, k]
+        tiles = [w0 * held(t, g0, k) + w1 * held(t, g1, k)
                  for k in range(win_y // 2 + 1)]
         main = split_dot(jnp.concatenate(tiles[:-1], axis=0), exp_ref[...])
         turned = [tiles[-1]] + [pltpu.roll(tiles[-1], depth - 4 * a, 1) for a in range(1, win_y)]
@@ -229,8 +276,7 @@
         low, w0, w1 = hat(j)
         return w0 * lines[low] + w1 * lines[low + 1]
 
-    @pl.loop(0, 2)
-    def _(t):
+    def ghosts(t):
         for x in range(planes):
             shift, w0, w1 = hat(x + 2)
             inner, outer = window_rows(t, me * (planes // 2) + shift, w0, w1, (0, 1))
@@ -251,8 +297,14 @@
         start[x, y] = value
         u_buf[following, x, y + 2] = value
 
+    ghosts(0)
+    gather_middle(gath_new, pay.at[1], 1)
     for substep in range(2):
         for section in range(4):
+            if substep == 0 and section == 1:
+                gather_last(gath_new, 1)
+                gather_end(gath_new, 1)
+                ghosts(1)
             t = 0.5 * (substep + fractions[section])
             ghost_rows(t)
             run_stage(section, 0.5 * coarse_step, near, far, t, fine_store)
@@ -264,23 +316,25 @@
         folded.append(start[0, 2 * y] + start[0, 2 * y + 1] + start[1, 2 * y] + start[1, 2 * y + 1])
     got = split_dot(jnp.concatenate(folded, axis=0), mean_ref[...])
     for t in range(half_y // 2):
-        means[t] = (got[2 * t * fields:(2 * t + 1) * fields]
+        sums[t] = (got[2 * t * fields:(2 * t + 1) * fields]
                     + pltpu.roll(got[(2 * t + 1) * fields:(2 * t + 2) * fields], half_z, 1))
-        landed[me, t] = means[t]
-    send_all(means, landed.at[me], 2)
+    gather_start(landed, sums, 2)
+    landed[core, pair] = sums[...]
+    gather_middle(landed, sums, 2)
 
     @pl.loop(0, rows)
     def _(y):
         for x in range(planes):
             out_ref[1, x, y] = start[x, y]
 
-    wait_all(means, landed.at[me], 2)
+    gather_last(landed, 2)
+    gather_end(landed, 2)
     distance = lax.rem(lanes - off_ref[2] + depth, depth)
     for x in range(planes):
         relative = lax.rem(me * planes + x - p + total, total)
         source = lax.rem(relative, half_x)
         for k in range(half_y // 2):
-            tile = landed[source, k]
+            tile = landed[lax.rem(source, 2), source // 2, k]
             placed = split_dot(tile, place_ref[...])
             for parity in range(2):
                 acc[0, 2 * k + parity] = placed[:, parity * depth:(parity + 1) * depth]
@@ -335,18 +389,21 @@
             pltpu.VMEM((2,) + block, f32),
             pltpu.VMEM(block, f32),
             pltpu.VMEM(block, f32),
-            pltpu.VMEM((2 * fields, 8 * fields), bf16),
+            pltpu.VMEM(block, f32),
+            pltpu.VMEM((2 * fields, 6 * fields), bf16),
+            pltpu.VMEM((2 * fields, 2 * fields), bf16),
             pltpu.VMEM((2, planes, win_tiles, fields, depth), f32),
-            pltpu.VMEM((2, n, planes, win_tiles, fields, depth), f32),
+            pltpu.VMEM((2, n // 2, planes, win_tiles, fields, depth), f32),
+            pltpu.VMEM((2, n // 2, planes, win_tiles, fields, depth), f32),
             pltpu.VMEM((2, planes, 4, fields, depth), f32),
             pltpu.VMEM((2,) + block, f32),
             pltpu.VMEM((2,) + block, f32),
             pltpu.VMEM((rows // 4, fields, depth), f32),
-            pltpu.VMEM((n, rows // 4, fields, depth), f32),
+            pltpu.VMEM((2, n // 2, rows // 4, fields, depth), f32),
             pltpu.SemaphoreType.DMA((2, 2)),
             pltpu.SemaphoreType.DMA((2, 2)),
-            pltpu.SemaphoreType.DMA((3, n)),
-            pltpu.SemaphoreType.DMA((3, n)),
+            pltpu.SemaphoreType.DMA((3, n // 4 + 1)),
+            pltpu.SemaphoreType.DMA((3, n // 4 + 1)),
         ],
         compiler_params=pltpu.CompilerParams(
             collective_id=0, has_side_effects=True, vmem_limit_bytes=48 * 1024 * 1024),

time: 277 us -> 208 us (0.75)
  Pallas kernels: 266 us -> 197 us
    pallas_call x1, Pallas kernels: 266 us -> 197 us  [local(): pl.pallas_call(lambda *refs: kernel(n, *refs), out_shape=jax.ShapeDtypeSt...]
where the time goes in v2:
time: 208 us; the launch traced here: 207 us
  Pallas kernels  197 us (95%)
  local copies, waits for them, and re-layouts  5.03 us (2%)
  other arithmetic  3.32 us (2%)
    pallas_call x1, Pallas kernels, local(): pl.pallas_call(lambda *refs: kernel(n, *refs), out_shape=jax.ShapeDtypeSt...  197 us

profile of v2, /device:TPU:13, one launch (start us, length us, event | category | flops | bytes accessed | tf_op | source)
XLA Modules:
  0.0 207.0 jit_solution(15431618786218178449)
XLA Ops:
  0.0 0.0 copy-start.1
  0.0 1.3 slice.15
  2.7 0.7 broadcast_compare_fusion
  3.4 0.7 and_select_fusion
  4.1 0.7 broadcast_in_dim.48.refs_2_
  4.9 0.1 select_convert_fusion.refs_7_
  5.0 0.8 copy.6
  5.8 0.8 fusion.4
  6.6 0.8 pad_maximum_fusion.2.refs_1_
  7.4 0.2 select_convert_fusion.1
  7.6 0.0 copy-done.1
  7.6 0.5 copy.10
  8.1 0.0 copy-start
  8.1 0.6 copy-done
  8.8 197.2 %shard_map.55 = f32[2,2,16,24,128]{4,3,2,1,0:T(8,128)S(1)} custom-call(s32[3]{0:T(128)S(1)} %copy-done, f32[24,96]{1,0:T(8,128)S(1)} %pad_maximum_fusion.2.refs_1_, f32[24,128]{1,0:T(8,128)S(1)} %broadcast_in_dim.48.refs_2_, f32[2,2,16,24,128]{4,3,2,1,0:T(8,128)S(1)} %bitcast.16, bf16[128,256]{1,0:T(8,128)(2,1)S(1)} %add_convert_fusion.refs_4_, ...), custom_call_target="tpu_custom_call" | custom-call | tf_op jit(solution)/shard_map/pallas_call | solution.py:381
  206.0 1.0 copy.8
  (16 shorter events, 0.2 us)
Async XLA Ops:
  0.0 7.6 %copy-start.1 = (f32[2,24,2,16,128]{4,3,2,1,0:T(8,128)S(1)}, f32[2,24,2,16,128]{4,3,2,1,0:T(8,128)}, u32[]{:S(2)}) copy-start(f32[2,24,2,16,128]{4,3,2,1,0:T(8,128)} %param.5) | copy-start | bytes 2359300
  8.1 0.7 copy-start

commit v3 on v2

--- a/solution.py
+++ b/solution.py
@@ -24,7 +24,7 @@
 
 
 def kernel(n, off_ref, mix_ref, diff_ref, lev_ref, zsel_ref, exp_ref, expx_ref, mean_ref, place_ref, out_ref,
-           u_buf, l_buf, r_buf, start, acc, part, weights, weights_x, pay, gath_old, gath_new, gy, gz, gx, sums, landed,
+           u_buf, l_buf, r_buf, start, acc, part, weights, weights_x, pay, gath_old, gath_new, gy, gz, gx, sums, landed, fine_in, fine_out,
            halo_send, halo_recv, all_send, all_recv):
     planes, rows, fields, depth = lev_ref.shape[1:]
     total = planes * n
@@ -42,6 +42,13 @@
 
     pl.semaphore_wait(barrier, n - 1)
 
+    def snake(d):
+        return d + lax.rem(d // 4, 2) * (2 - 4 * lax.rem(d // 2, 2))
+
+    pos = snake(me)
+    turned_row = lax.rem(me // 4, 2) == 1
+    straight_row = lax.rem(me // 4, 2) == 0
+    level = [0]
     core = lax.rem(me, 2)
     pair = me // 2
     across = me + 2 - 4 * lax.rem(pair, 2)
@@ -77,9 +84,14 @@
 
     def halo(slot):
         copies = []
-        for side, target, dst in ((0, right, l_buf), (1, left, r_buf)):
+        base = slot
+        slot = slot + 2 * level[0]
+        ends = ((0, right, l_buf), (1, left, r_buf))
+        if level[0]:
+            ends = ((0, snake(lax.rem(pos + 1, n)), l_buf), (1, snake(lax.rem(pos + n - 1, n)), r_buf))
+        for side, target, dst in ends:
             copies.append(pltpu.make_async_remote_copy(
-                src_ref=u_buf.at[slot, :, pl.ds(2, rows)], dst_ref=dst.at[slot],
+                src_ref=u_buf.at[base, :, pl.ds(2, rows)], dst_ref=dst.at[slot],
                 send_sem=halo_send.at[slot, side], recv_sem=halo_recv.at[slot, side],
                 device_id={"space": target}, device_id_type=pl.DeviceIdType.MESH))
         return copies
@@ -130,7 +142,7 @@
         copies = halo(slot)
         for copy in copies:
             copy.start()
-        if stage[0] > 0:
+        if stage[0] not in (0, 4):
             for copy in halo(following):
                 copy.wait_send()
         def product(stacks, factor):
@@ -170,16 +182,17 @@
             copy.wait_recv()
         if t is not None:
             for edge, buf in ((0, l_buf), (n - 1, r_buf)):
-                @pl.when(me == edge)
+                @pl.when(pos == edge)
                 def _(buf=buf):
                     @pl.loop(0, rows)
                     def _(y):
                         for x in range(planes):
-                            buf[slot, x, y] = blend(lambda i: gx[i, x, y], t)
+                            buf[slot + 2, x, y] = blend(lambda i: gx[i, x, y], t)
 
         def body(y, carry):
-            line = [l_buf[slot, 0, y], l_buf[slot, 1, y], u_buf[slot, 0, y + 2], u_buf[slot, 1, y + 2],
-                    r_buf[slot, 0, y], r_buf[slot, 1, y]]
+            there = slot + 2 * level[0]
+            line = [l_buf[there, 0, y], l_buf[there, 1, y], u_buf[slot, 0, y + 2], u_buf[slot, 1, y + 2],
+                    r_buf[there, 0, y], r_buf[there, 1, y]]
             stacks, even = [], []
             for x in range(planes):
                 m2, m1, p1, p2 = line[x], line[x + 1], line[x + 3], line[x + 4]
@@ -215,6 +228,17 @@
                 row = k if k < 2 else rows + k
                 u_buf[slot, x, row] = blend(lambda i: gy[i, x, k], t)
 
+    @pl.when(turned_row)
+    def _():
+        remote(lev_ref.at[1], fine_in, 3, 0, across).start()
+
+    @pl.when(straight_row)
+    def _():
+        @pl.loop(0, rows)
+        def _(y):
+            for x in range(planes):
+                fine_in[x, y] = lev_ref[1, x, y]
+
     near, far = set_weights(1.0)
 
     @pl.loop(0, rows)
@@ -243,13 +267,20 @@
     gath_new[core, pair] = pay[1]
 
     near, far = set_weights(0.5)
+    for copy in halo(1 - stage[0] % 2):
+        copy.wait_send()
+    level[0] = 1
+
+    @pl.when(turned_row)
+    def _():
+        remote(lev_ref.at[1], fine_in, 3, 0, across).wait()
 
     @pl.loop(0, rows)
     def _(y):
         for x in range(planes):
             out_ref[0, x, y] = start[x, y]
-            start[x, y] = lev_ref[1, x, y]
-            u_buf[stage[0] % 2, x, y + 2] = lev_ref[1, x, y]
+            start[x, y] = fine_in[x, y]
+            u_buf[stage[0] % 2, x, y + 2] = fine_in[x, y]
 
     gather_end(gath_old, 0)
 
@@ -279,13 +310,13 @@
     def ghosts(t):
         for x in range(planes):
             shift, w0, w1 = hat(x + 2)
-            inner, outer = window_rows(t, me * (planes // 2) + shift, w0, w1, (0, 1))
+            inner, outer = window_rows(t, pos * (planes // 2) + shift, w0, w1, (0, 1))
             for k in range(4):
                 gy[t, x, k] = mix_rows(inner, k if k < 2 else rows + k)
             for y in range(rows):
                 gz[t, x, y] = mix_rows(outer, y + 2)
         for edge, base in ((0, 0), (n - 1, total + 2)):
-            @pl.when(me == edge)
+            @pl.when(pos == edge)
             def _(base=base):
                 for x in range(2):
                     low, w0, w1 = hat(base + x)
@@ -311,6 +342,10 @@
     for copy in halo(1 - stage[0] % 2):
         copy.wait_send()
 
+    @pl.when(turned_row)
+    def _():
+        remote(start, fine_out, 4, 0, across).start()
+
     folded = []
     for y in range(half_y):
         folded.append(start[0, 2 * y] + start[0, 2 * y + 1] + start[1, 2 * y] + start[1, 2 * y + 1])
@@ -322,17 +357,28 @@
     landed[core, pair] = sums[...]
     gather_middle(landed, sums, 2)
 
-    @pl.loop(0, rows)
-    def _(y):
-        for x in range(planes):
-            out_ref[1, x, y] = start[x, y]
-
     gather_last(landed, 2)
     gather_end(landed, 2)
+    @pl.when(straight_row)
+    def _():
+        @pl.loop(0, rows)
+        def _(y):
+            for x in range(planes):
+                out_ref[1, x, y] = start[x, y]
+
+    @pl.when(turned_row)
+    def _():
+        remote(start, fine_out, 4, 0, across).wait()
+
+        @pl.loop(0, rows)
+        def _(y):
+            for x in range(planes):
+                out_ref[1, x, y] = fine_out[x, y]
+
     distance = lax.rem(lanes - off_ref[2] + depth, depth)
     for x in range(planes):
         relative = lax.rem(me * planes + x - p + total, total)
-        source = lax.rem(relative, half_x)
+        source = snake(lax.rem(relative, half_x))
         for k in range(half_y // 2):
             tile = landed[lax.rem(source, 2), source // 2, k]
             placed = split_dot(tile, place_ref[...])
@@ -385,8 +431,8 @@
         out_specs=vmem,
         scratch_shapes=[
             pltpu.VMEM((2, planes, rows + 4, fields, depth), f32),
-            pltpu.VMEM((2,) + block, f32),
-            pltpu.VMEM((2,) + block, f32),
+            pltpu.VMEM((4,) + block, f32),
+            pltpu.VMEM((4,) + block, f32),
             pltpu.VMEM(block, f32),
             pltpu.VMEM(block, f32),
             pltpu.VMEM(block, f32),
@@ -400,10 +446,12 @@
             pltpu.VMEM((2,) + block, f32),
             pltpu.VMEM((rows // 4, fields, depth), f32),
             pltpu.VMEM((2, n // 2, rows // 4, fields, depth), f32),
-            pltpu.SemaphoreType.DMA((2, 2)),
-            pltpu.SemaphoreType.DMA((2, 2)),
-            pltpu.SemaphoreType.DMA((3, n // 4 + 1)),
-            pltpu.SemaphoreType.DMA((3, n // 4 + 1)),
+            pltpu.VMEM(block, f32),
+            pltpu.VMEM(block, f32),
+            pltpu.SemaphoreType.DMA((4, 2)),
+            pltpu.SemaphoreType.DMA((4, 2)),
+            pltpu.SemaphoreType.DMA((5, n // 4 + 1)),
+            pltpu.SemaphoreType.DMA((5, n // 4 + 1)),
         ],
         compiler_params=pltpu.CompilerParams(
             collective_id=0, has_side_effects=True, vmem_limit_bytes=48 * 1024 * 1024),

time: 208 us -> 222 us (1.067)
  Pallas kernels: 197 us -> 211 us
    pallas_call x1, Pallas kernels: 197 us -> 211 us  [local(): pl.pallas_call(lambda *refs: kernel(n, *refs), out_shape=jax.ShapeDtypeSt...]
where the time goes in v3:
time: 222 us; the launch traced here: 221 us
  Pallas kernels  211 us (95%)
  local copies, waits for them, and re-layouts  5.03 us (2%)
  other arithmetic  3.32 us (1%)
    pallas_call x1, Pallas kernels, local(): pl.pallas_call(lambda *refs: kernel(n, *refs), out_shape=jax.ShapeDtypeSt...  211 us

profile of v3, /device:TPU:13, one launch (start us, length us, event | category | flops | bytes accessed | tf_op | source)
XLA Modules:
  0.0 220.7 jit_solution(13556864036103647338)
XLA Ops:
  0.0 0.0 copy-start.1
  0.0 1.3 slice.15
  2.7 0.7 broadcast_compare_fusion
  3.4 0.7 and_select_fusion
  4.1 0.7 broadcast_in_dim.48.refs_2_
  4.9 0.1 select_convert_fusion.refs_7_
  5.0 0.8 copy.6
  5.8 0.8 fusion.4
  6.6 0.8 pad_maximum_fusion.2.refs_1_
  7.4 0.2 select_convert_fusion.1
  7.6 0.0 copy-done.1
  7.6 0.5 copy.10
  8.1 0.0 copy-start
  8.1 0.6 copy-done
  8.8 210.9 %shard_map.55 = f32[2,2,16,24,128]{4,3,2,1,0:T(8,128)S(1)} custom-call(s32[3]{0:T(128)S(1)} %copy-done, f32[24,96]{1,0:T(8,128)S(1)} %pad_maximum_fusion.2.refs_1_, f32[24,128]{1,0:T(8,128)S(1)} %broadcast_in_dim.48.refs_2_, f32[2,2,16,24,128]{4,3,2,1,0:T(8,128)S(1)} %bitcast.16, bf16[128,256]{1,0:T(8,128)(2,1)S(1)} %add_convert_fusion.refs_4_, ...), custom_call_target="tpu_custom_call" | custom-call | tf_op jit(solution)/shard_map/pallas_call | solution.py:427
  219.6 1.0 copy.8
  (16 shorter events, 0.2 us)
Async XLA Ops:
  0.0 7.6 %copy-start.1 = (f32[2,24,2,16,128]{4,3,2,1,0:T(8,128)S(1)}, f32[2,24,2,16,128]{4,3,2,1,0:T(8,128)}, u32[]{:S(2)}) copy-start(f32[2,24,2,16,128]{4,3,2,1,0:T(8,128)} %param.5) | copy-start | bytes 2359300
  8.1 0.7 copy-start
